TPU v7x, 32 devices: a whole 2x2x4 slice. The times are simulated.
32 devices in a mesh: seq: 8 (over z, y), head: 4 (over x, core).
Axes of the slice: x: 2, y: 2, z: 4, core: 2. Of those that a mesh axis runs over, the one named last changes fastest.
Arguments:
- inputs: bfloat16 [2048, 5120], P('seq', 'head'), may hold values from -6 to 6
- time_step: float32 [80, 2048], P('head', 'seq'), may hold values from 0.01 to 0.3
- decay_rate: float32 [80], P('head'), may hold values from 0.0001 to 1
- input_map: bfloat16 [2048, 128], P('seq'), may hold values from -6 to 6
- output_map: bfloat16 [2048, 128], P('seq'), may hold values from -0.59765625 to 0.59765625
- output_grad: bfloat16 [2048, 5120], P('seq', 'head'), may hold values from -3 to 3
- span_states: float32 [8, 80, 64, 128], P('seq', 'head'), may hold values from -6 to 6
- resets: int32 [8], P('seq'), may hold values from 0 to 4095
Outputs:
- grad_inputs: bfloat16 [2048, 5120], P('seq', 'head')
- grad_input_map: float32 [2048, 128], P('seq')
- grad_rate: float32 [80], P('head')
Inputs may be any that keep to these rules, and one draw needn't show every extreme that they name: `resets`: A value p under 256 means that a document starts at position p of that span; a value of 256 or more means that none starts in it.
All inputs are finite; a program needn't handle non-finite values.
Results may differ from a plain program's by a relative error of at most 0.003.
Values sent between devices are 32-bit elements; how exact they have to be, the bound alone decides.
A program may use at most 64 MiB of HBM per device.

v0:
```python
import jax
import jax.numpy as jnp
from jax import lax
from jax.sharding import PartitionSpec as P

highest = lax.Precision.HIGHEST


def prepare(x_block, step_block, decay_rate, b_block, c_block, grad_block, start_state, reset_at):
    block_len = step_block.shape[1]
    positions = jnp.arange(block_len, dtype=jnp.int32)
    later_doc = positions >= reset_at
    no_reset = reset_at >= block_len
    elapsed = jnp.cumsum(step_block, axis=1)
    log_decay = -decay_rate[:, None] * elapsed
    joined = (later_doc[:, None] == later_doc[None, :]) & (positions[None, :] >= positions[:, None])
    log_gaps = log_decay[:, None, :] - log_decay[:, :, None]
    pair_weight = jnp.where(joined[None], jnp.exp(jnp.where(joined[None], log_gaps, 0.0)), 0.0)
    intersection = jnp.dot(b_block, c_block.T, preferred_element_type=jnp.float32)
    products = jnp.einsum("shp,uhp->hsu", x_block, grad_block, preferred_element_type=jnp.float32)
    mixing = (pair_weight * intersection[None]).astype(jnp.bfloat16)
    pair_terms = pair_weight * products
    paired = pair_terms.astype(jnp.bfloat16)
    dx_inner = jnp.einsum("hsu,uhp->shp", mixing, grad_block, preferred_element_type=jnp.float32)
    db_inner = jnp.einsum("hsu,un->hsn", paired, c_block, preferred_element_type=jnp.float32)
    start_weight = jnp.where(later_doc[None], 0.0, jnp.exp(log_decay))
    end_weight = jnp.where(
        (later_doc | no_reset)[None], jnp.exp(log_decay[:, -1:] - log_decay), 0.0
    )
    carry_gain = jnp.where(no_reset, jnp.exp(log_decay[:, -1]), 0.0)
    c_wide = c_block.astype(jnp.float32)
    grad_wide = grad_block.astype(jnp.float32)
    weighted_c = start_weight[:, :, None] * c_wide[None]
    boundary_grad = jnp.einsum("hun,uhp->hpn", weighted_c, grad_wide, precision=highest)
    state_read = jnp.einsum("uhp,hpn->hun", grad_wide, start_state, precision=highest)
    start_term = jnp.sum(state_read * c_wide[None], axis=2)
    inside_term = jnp.sum(
        pair_terms
        * intersection[None]
        * step_block[:, :, None]
        * (elapsed[:, None, :] - elapsed[:, :, None]),
        axis=(1, 2),
    )
    entry_term = jnp.sum(start_weight * elapsed * start_term, axis=1)
    return (
        carry_gain,
        boundary_grad,
        dx_inner,
        db_inner,
        inside_term + entry_term,
        end_weight,
        elapsed,
    )


def finish(prepared, x_block, step_block, b_block, start_state, carried):
    carry_gain, boundary_grad, dx_inner, db_inner, partial_rate, end_weight, elapsed = prepared
    b_wide = b_block.astype(jnp.float32)
    x_wide = x_block.astype(jnp.float32)
    carried_b = jnp.einsum("sn,hpn->shp", b_wide, carried, precision=highest)
    carried_x = jnp.einsum("shp,hpn->hsn", x_wide, carried, precision=highest)
    step_rows = step_block.T[:, :, None]
    end_rows = end_weight.T[:, :, None]
    grad_x = (step_rows * (dx_inner + end_rows * carried_b)).astype(jnp.bfloat16)
    grad_b = jnp.sum(
        step_block[:, :, None] * (db_inner + end_weight[:, :, None] * carried_x), axis=0
    )
    last_elapsed = elapsed[:, -1]
    leaving_term = jnp.sum(
        end_weight
        * step_block
        * (last_elapsed[:, None] - elapsed)
        * jnp.sum(carried_x * b_wide[None], axis=2),
        axis=1,
    )
    through_term = carry_gain * last_elapsed * jnp.sum(carried * start_state, axis=(1, 2))
    return (grad_x, grad_b, partial_rate + leaving_term + through_term)


def backward_step(running, members):
    grad_piece, gain_piece = members
    return (grad_piece + gain_piece[:, None] * running, running)


def body(inputs, time_step, decay_rate, input_map, output_map, output_grad, span_states, resets):
    length = time_step.shape[1]
    block_count = span_states.shape[0]
    block_len = length // block_count
    head_count = decay_rate.shape[0]
    head_width = inputs.shape[1] // head_count
    number = 0
    x_block = inputs.reshape(block_len, head_count, head_width)
    grad_block = output_grad.reshape(block_len, head_count, head_width)
    step_block = time_step
    b_block = input_map
    prepared = prepare(
        x_block,
        step_block,
        decay_rate,
        b_block,
        output_map,
        grad_block,
        span_states[number],
        resets[number],
    )
    pieces = [(prepared, x_block, step_block, b_block)]
    gain_total = jnp.ones((head_count,), jnp.float32)
    grad_total = jnp.zeros_like(span_states[0])
    for number in reversed(range(block_count)):
        gain_block, grad_block_sum = (pieces[number][0][0], pieces[number][0][1])
        grad_total = grad_block_sum + gain_block[:, None, None] * grad_total
        gain_total = gain_block * gain_total
    seq_count = lax.axis_size("seq")
    entries = grad_total.shape[1] * grad_total.shape[2]
    sliced = grad_total.reshape(head_count, seq_count, entries // seq_count)
    received = lax.all_to_all(sliced, "seq", split_axis=1, concat_axis=1, tiled=True)
    gains = lax.all_gather(gain_total[None], "seq", axis=0, tiled=True)
    ending, exclusive = lax.scan(
        backward_step,
        jnp.zeros_like(received[:, 0]),
        (jnp.transpose(received, (1, 0, 2)), gains),
        reverse=True,
    )
    returned = lax.all_to_all(
        jnp.transpose(exclusive, (1, 0, 2)), "seq", split_axis=1, concat_axis=1, tiled=True
    )
    incoming = returned.reshape(grad_total.shape)
    carried = incoming
    grad_x_list = [None] * block_count
    grad_b_list = [None] * block_count
    rate_total = jnp.zeros((head_count,), jnp.float32)
    for number in reversed(range(block_count)):
        prepared, x_block, step_block, b_block = pieces[number]
        grad_x, grad_b, rate_part = finish(
            prepared, x_block, step_block, b_block, span_states[number], carried
        )
        grad_x_list[number] = grad_x.reshape(block_len, head_count * head_width)
        grad_b_list[number] = grad_b
        rate_total = rate_part
        carried = prepared[1] + prepared[0][:, None, None] * carried
    grad_inputs = grad_x_list[0]
    grad_input_map = lax.psum(grad_b_list[0], "head")
    grad_rate = -lax.psum(rate_total, "seq")
    return (grad_inputs, grad_input_map, grad_rate)


def solution(mesh):
    in_specs = (
        P("seq", "head"),
        P("head", "seq"),
        P("head"),
        P("seq", None),
        P("seq", None),
        P("seq", "head"),
        P("seq", "head", None, None),
        P("seq"),
    )
    out_specs = (P("seq", "head"), P("seq", None), P("head"))
    return jax.shard_map(body, mesh=mesh, in_specs=in_specs, out_specs=out_specs, check_vma=False)
```

profile of v0, /device:TPU:0, one launch (start us, length us, event | category | flops | bytes accessed | tf_op | source)
XLA Modules:
  0.0 141.0 jit_solution(17333116644024165966)
XLA Ops:
  8.0 0.7 neg.7
  8.6 0.8 reshape.290
  9.4 0.6 reduce-window.6
  10.0 0.2 slice_reduce_fusion
  10.3 0.6 iota_compare_fusion.1
  10.9 0.1 exponential_select_fusion.2
  11.0 0.2 select_reduce_fusion
  11.2 0.9 copy.37
  12.2 1.4 copy.36
  13.6 1.7 %fusion.31 = f32[20,64,128]{2,1,0:T(8,128)S(1)} fusion(bf16[256,20,64]{0,2,1:T(8,128)(2,1)S(1)} %bitcast.80, f32[256,128]{0,1:T(8,128)S(1)} %copy.37, f32[20,256]{1,0:T(8,128)S(1)} %get-tuple-element.152, f32[20]{0:T(128)S(1)} %broadcast_multiply_fusion.1), kind=kOutput, calls=%fused_computation.38 | convolution fusion | flops 504135680 | bytes 1462352 | tf_op jit(solution)/shard_map/hun,uhp->hpn/dot_general | solution.py:34
  15.3 0.1 reshape.293
  15.4 1.3 copy.39
  16.7 7.3 %all-to-all-start = ((f32[20,8,1024]{2,0,1:T(8,128)}), f32[20,8,1024]{2,0,1:T(8,128)S(1)}, u32[]{:S(2)}, u32[]{:S(2)}) async-start(f32[20,8,1024]{2,0,1:T(8,128)} %copy.39), calls=%async_computation | async-start | bytes 1572864 | tf_op jit(solution)/shard_map/all_to_all | solution.py:116
  24.0 0.6 dynamic-slice
  25.3 0.2 dynamic-update-slice
  25.6 26.1 %all-reduce = f32[160]{0:T(256)S(1)} all-reduce(f32[160]{0:T(256)S(1)} %dynamic-update-slice), channel_id=2, replica_groups=mesh['seq'=8,'head'=4] {'seq'}, use_global_device_ids=true, to_apply=%add | all-reduce | flops 160 | bytes 1280
  51.7 0.7 reshape.297
  52.3 0.7 convert_element_type.21
  53.0 0.2 copy.41
  53.3 0.1 squeeze.25
  53.4 0.6 compare_bitcast_fusion
  53.9 0.7 slice_reduce_fusion.1
  54.7 1.4 %fusion.37 = pred[256,256]{1,0:T(8,128)(4,1)} fusion(pred[256]{0:T(512)(128)(4,1)} %copy-done.10), kind=kLoop, calls=%fused_computation.42 | loop fusion | flops 196608 | bytes 65792 | tf_op jit(solution)/shard_map/and | solution.py:16
  56.1 1.8 %fusion.43 = f32[256,256]{1,0:T(8,128)} fusion(bf16[256,128]{1,0:T(8,128)(2,1)} %param.13, bf16[256,128]{1,0:T(8,128)(2,1)} %param.14), kind=kOutput, calls=%fused_computation.64 | convolution fusion | flops 16777216 | bytes 393216 | tf_op jit(solution)/shard_map/dot_general | solution.py:19
  57.9 1.0 broadcast_in_dim.97
  58.9 11.4 %while.17 = (s32[]{:T(128)}, f32[20,1024]{1,0:T(8,128)S(1)}, f32[8,20,1024]{2,1,0:T(8,128)}, f32[8,20,1024]{2,1,0:T(8,128)S(1)}, f32[8,20]{1,0:T(8,128)}, /*index=5*/s32[]{:T(128)}, s32[]{:T(128)}, s32[]{:T(128)}) while((s32[]{:T(128)}, f32[20,1024]{1,0:T(8,128)S(1)}, f32[8,20,1024]{2,1,0:T(8,128)}, f32[8,20,1024]{2,1,0:T(8,128)S(1)}, ...), condition=%wide.region_3.4_spmd.clone, body=%wide.region_2.3_spmd.clone.sunk | while | flops 81924 | bytes 426352 | solution.py:118
  58.9 0.7 fusion.55
  59.5 0.6 bitcast_dynamic-update-slice_fusion.2
  60.2 0.1 bitcast_add_fusion.2
  60.3 0.7 fusion.55
  61.0 0.6 bitcast_dynamic-update-slice_fusion.2
  61.6 0.1 bitcast_add_fusion.2
  61.7 0.7 fusion.55
  62.4 0.6 bitcast_dynamic-update-slice_fusion.2
  63.0 0.1 bitcast_add_fusion.2
  63.1 0.7 fusion.55
  63.8 0.6 bitcast_dynamic-update-slice_fusion.2
  64.5 0.1 bitcast_add_fusion.2
  64.6 0.7 fusion.55
  65.2 0.6 bitcast_dynamic-update-slice_fusion.2
  65.9 0.1 bitcast_add_fusion.2
  66.0 0.7 fusion.55
  66.7 0.6 bitcast_dynamic-update-slice_fusion.2
  67.3 0.1 bitcast_add_fusion.2
  67.4 0.7 fusion.55
  68.1 0.6 bitcast_dynamic-update-slice_fusion.2
  68.9 0.7 fusion.55
  69.5 0.6 bitcast_dynamic-update-slice_fusion.2
  70.3 4.5 %all-to-all-start.1 = ((f32[20,8,1024]{2,0,1:T(8,128)}), f32[20,8,1024]{2,0,1:T(8,128)S(1)}, u32[]{:S(2)}, u32[]{:S(2)}) async-start(f32[20,8,1024]{2,0,1:T(8,128)} %bitcast.8), calls=%async_computation.1 | async-start | bytes 1572864 | tf_op jit(solution)/shard_map/all_to_all | solution.py:124
  74.8 2.8 %multiply_reduce_fusion.1 = f32[20,256]{1,0:T(8,128)} fusion(bf16[256,20,64]{0,2,1:T(8,128)(2,1)S(1)} %bitcast.81, f32[256,128]{0,1:T(8,128)} %copy-done.7, f32[1,20,64,128]{3,2,1,0:T(8,128)S(1)} %copy-done.2), kind=kOutput, calls=%fused_computation.17 | convolution fusion | flops 504622080 | bytes 1462272 | tf_op jit(solution)/shard_map/uhp,hpn->hun/dot_general | solution.py:35
  77.7 3.7 %fusion.21 = f32[256,20,64]{0,2,1:T(8,128)} fusion(bf16[256,20,64]{0,2,1:T(8,128)(2,1)S(1)} %bitcast.82, f32[256,256]{1,0:T(8,128)} %fusion.43, f32[20,256]{1,0:T(8,128)S(1)} %get-tuple-element.153, pred[256,256]{1,0:T(8,128)(4,1)} %fusion.37), kind=kOutput, calls=%fused_computation.29 | convolution fusion | flops 174325760 | bytes 2314240 | tf_op jit(solution)/shard_map/hsu,uhp->shp/dot_general | solution.py:24
  81.4 5.3 %multiply_reduce_fusion = (f32[20]{0:T(128)}, f32[20,256,256]{2,1,0:T(8,128)}) fusion(f32[20,256]{1,0:T(8,128)S(1)} %bitcast.86, f32[20,256]{1,0:T(8,128)S(1)} %copy-done.6, f32[256,256]{1,0:T(8,128)S(1)} %copy-done.5, f32[20,256]{1,0:T(8,128)S(1)} %get-tuple-element.153, pred[256,256]{1,0:T(8,128)(4,1)S(1)} %copy-done.8, ...), kind=kOutput, calls=%fused_computation.4 | convolution fusion | flops 179568624 | bytes 6942800 | tf_op jit(solution)/shard_map/shp,uhp->hsu/dot_general | solution.py:20
  86.8 5.5 %all-to-all-done.1 = f32[20,8,1024]{2,0,1:T(8,128)S(1)} async-done(((f32[20,8,1024]{2,0,1:T(8,128)}), f32[20,8,1024]{2,0,1:T(8,128)S(1)}, u32[]{:S(2)}, u32[]{:S(2)}) %all-to-all-start.1) | async-done | bytes 655392 | tf_op jit(solution)/shard_map/all_to_all | solution.py:124
  92.3 1.1 multiply_reduce_fusion.2
  93.3 0.1 reshape.294
  93.4 2.8 %fusion.9 = (f32[20,256]{1,0:T(8,128)S(1)}, f32[20,128,256]{1,2,0:T(8,128)S(1)}) fusion(f32[256,128]{1,0:T(8,128)} %convert_element_type.21, f32[20,64,128]{2,1,0:T(8,128)S(1)} %reshape.294, bf16[256,20,64]{0,2,1:T(8,128)(2,1)S(1)} %bitcast.77), kind=kOutput, calls=%fused_computation.16 | convolution fusion | flops 504622080 | bytes 4083712 | tf_op jit(solution)/shard_map/shp,hpn->hsn/dot_general | solution.py:61
  96.3 0.2 multiply_reduce_fusion.4
  96.5 5.2 %fusion.8 = f32[256,128]{1,0:T(8,128)} fusion(f32[20,128,256]{1,2,0:T(8,128)S(1)} %get-tuple-element.155, f32[20,256]{1,0:T(8,128)S(1)} %get-tuple-element.150, f32[20,256]{1,0:T(8,128)S(1)} %copy-done.6, f32[20,256,256]{2,1,0:T(8,128)} %get-tuple-element.157, f32[20,256]{1,0:T(8,128)S(1)} %get-tuple-element.153, pred[256,256]{1,0:T(8,128)(4,1)} %fusion.37, ...), kind=kOutput, calls=%fused_computation.15 | convolution fusion | flops 344686592 | bytes 8187904 | tf_op jit(solution)/shard_map/hsu,un->hsn/dot_general | solution.py:25
  101.8 0.7 fusion.25
  102.4 19.4 %psum.15 = f32[20]{0:T(128)S(1)} all-reduce(f32[20]{0:T(128)S(1)} %multiply_add_fusion), channel_id=1, replica_groups=mesh['seq'=8,'head'=4] {'seq'}, use_global_device_ids=true, to_apply=%region_12.13 | all-reduce | flops 20 | bytes 160 | tf_op jit(solution)/shard_map/psum | solution.py:143
  121.8 1.1 copy.44
  122.9 0.5 neg.8
  123.4 9.1 %all-reduce.3.cloned.1.call-done = f32[256,128]{1,0:T(8,128)} async-done(((f32[256,128]{1,0:T(8,128)}), f32[256,128]{1,0:T(8,128)}) %all-reduce.3.cloned.1.call-update) | async-done | bytes 131088 | tf_op jit(solution)/shard_map/psum | solution.py:142
  132.6 1.6 %copy.62 = f32[256,128]{1,0:T(8,128)} copy(f32[256,128]{1,0:T(8,128)} %all-reduce.3.cloned.1.call-done) | data formatting | bytes 262144
  (58 shorter events, 0.5 us)
Async XLA Ops:
  7.2 16.8 %copy-start.20 = (u32[32]{0:T(128)S(1)}, u32[32]{0:T(128)}, u32[]{:S(2)}) copy-start(u32[32]{0:T(128)} %constant.57) | copy-start | bytes 388
  7.2 45.2 %copy-start.3 = (bf16[256,128]{1,0:T(8,128)(2,1)S(1)}, bf16[256,128]{1,0:T(8,128)(2,1)}, u32[]{:S(2)}) copy-start(bf16[256,128]{1,0:T(8,128)(2,1)} %param.13) | copy-start | bytes 196612
  7.2 45.8 %copy-start.1 = (bf16[256,1280]{1,0:T(8,128)(2,1)S(1)}, bf16[256,1280]{1,0:T(8,128)(2,1)}, u32[]{:S(2)}) copy-start(bf16[256,1280]{1,0:T(8,128)(2,1)} %param.10) | copy-start | bytes 1966084
  7.2 46.0 %copy-start.2 = (f32[1,20,64,128]{3,2,1,0:T(8,128)S(1)}, f32[1,20,64,128]{3,2,1,0:T(8,128)}, u32[]{:S(2)}) copy-start(f32[1,20,64,128]{3,2,1,0:T(8,128)} %param.16) | copy-start | bytes 1966084
  8.6 43.7 %copy-start.14 = (f32[20]{0:T(128)}, f32[20]{0:T(128)S(1)}, u32[]{:S(2)}) copy-start(f32[20]{0:T(128)S(1)} %neg.7) | copy-start | bytes 244
  10.9 41.4 %copy-start.10 = (pred[256]{0:T(512)(128)(4,1)}, pred[256]{0:T(512)(128)(4,1)S(1)}, u32[]{:S(2)}) copy-start(pred[256]{0:T(512)(128)(4,1)S(1)} %get-tuple-element.158) | copy-start | bytes 772
  11.2 41.1 %copy-start.11 = (f32[20]{0:T(128)}, f32[20]{0:T(128)S(1)}, u32[]{:S(2)}) copy-start(f32[20]{0:T(128)S(1)} %get-tuple-element.137) | copy-start | bytes 244
  12.2 1.4 copy-start.7
  16.7 41.2 %all-to-all-start = ((f32[20,8,1024]{2,0,1:T(8,128)}), f32[20,8,1024]{2,0,1:T(8,128)S(1)}, u32[]{:S(2)}, u32[]{:S(2)}) async-start(f32[20,8,1024]{2,0,1:T(8,128)} %copy.39), calls=%async_computation | async-start | bytes 1572864 | tf_op jit(solution)/shard_map/all_to_all | solution.py:116
  70.3 22.0 %all-to-all-start.1 = ((f32[20,8,1024]{2,0,1:T(8,128)}), f32[20,8,1024]{2,0,1:T(8,128)S(1)}, u32[]{:S(2)}, u32[]{:S(2)}) async-start(f32[20,8,1024]{2,0,1:T(8,128)} %bitcast.8), calls=%async_computation.1 | async-start | bytes 1572864 | tf_op jit(solution)/shard_map/all_to_all | solution.py:124
  74.8 57.8 %all-reduce.3.cloned.1.call-start = ((), (), s32[]{:S(2)}) async-start(), calls=%async_computation.2 | async-start | bytes 262144 | tf_op jit(solution)/shard_map/psum | solution.py:142
  77.7 3.7 %copy-start.5 = (f32[256,256]{1,0:T(8,128)S(1)}, f32[256,256]{1,0:T(8,128)}, u32[]{:S(2)}) copy-start(f32[256,256]{1,0:T(8,128)} %fusion.43) | copy-start | bytes 786436
  77.7 3.7 %copy-start.6 = (f32[20,256]{1,0:T(8,128)S(1)}, f32[20,256]{1,0:T(8,128)}, u32[]{:S(2)}) copy-start(f32[20,256]{1,0:T(8,128)} %param.11) | copy-start | bytes 61444
  77.7 3.7 %copy-start.8 = (pred[256,256]{1,0:T(8,128)(4,1)S(1)}, pred[256,256]{1,0:T(8,128)(4,1)}, u32[]{:S(2)}) copy-start(pred[256,256]{1,0:T(8,128)(4,1)} %fusion.37) | copy-start | bytes 196612
  86.8 9.4 %copy-start.9 = (f32[20,256]{1,0:T(8,128)S(1)}, f32[20,256]{1,0:T(8,128)}, u32[]{:S(2)}) copy-start(f32[20,256]{1,0:T(8,128)} %multiply_reduce_fusion.1) | copy-start | bytes 61444
  86.8 9.4 %copy-start.12 = (f32[20]{0:T(128)S(1)}, f32[20]{0:T(128)}, u32[]{:S(2)}) copy-start(f32[20]{0:T(128)} %copy-done.11) | copy-start | bytes 244
  86.8 9.5 %copy-start.13 = (f32[20]{0:T(128)S(1)}, f32[20]{0:T(128)}, u32[]{:S(2)}) copy-start(f32[20]{0:T(128)} %slice_reduce_fusion.1) | copy-start | bytes 244
  86.8 9.5 %copy-start.15 = (f32[20]{0:T(128)S(1)}, f32[20]{0:T(128)}, u32[]{:S(2)}) copy-start(f32[20]{0:T(128)} %copy-done.14) | copy-start | bytes 244
  86.8 9.5 %copy-start.16 = (pred[256]{0:T(512)(128)(4,1)S(1)}, pred[256]{0:T(512)(128)(4,1)}, u32[]{:S(2)}) copy-start(pred[256]{0:T(512)(128)(4,1)} %get-tuple-element.159) | copy-start | bytes 772
  86.8 9.5 %copy-start.18 = (pred[256]{0:T(512)(128)(4,1)S(1)}, pred[256]{0:T(512)(128)(4,1)}, u32[]{:S(2)}) copy-start(pred[256]{0:T(512)(128)(4,1)} %compare_bitcast_fusion) | copy-start | bytes 772
  96.5 5.2 %copy-start.17 = (f32[20]{0:T(128)S(1)}, f32[20]{0:T(128)}, u32[]{:S(2)}) copy-start(f32[20]{0:T(128)} %get-tuple-element.148) | copy-start | bytes 244
  96.5 5.2 %copy-start.19 = (f32[20]{0:T(128)S(1)}, f32[20]{0:T(128)}, u32[]{:S(2)}) copy-start(f32[20]{0:T(128)} %get-tuple-element.156) | copy-start | bytes 244
  96.5 5.2 %copy-start = (f32[256,20,64]{0,2,1:T(8,128)S(1)}, f32[256,20,64]{0,2,1:T(8,128)}, u32[]{:S(2)}) copy-start(f32[256,20,64]{0,2,1:T(8,128)} %fusion.21) | copy-start | bytes 3932164
  96.5 5.2 %copy-start.4 = (bf16[256,128]{1,0:T(8,128)(2,1)S(1)}, bf16[256,128]{1,0:T(8,128)(2,1)}, u32[]{:S(2)}) copy-start(bf16[256,128]{1,0:T(8,128)(2,1)} %param.13) | copy-start | bytes 196612
Sparse Core Ops, SparseCore 0:
  101.8 30.7 all-reduce.2
where the time goes:
time: 142 us; the launch traced here: 141 us
  blocking collectives  45.5 us (32%)
  matrix products  24 us (17%)
  local copies, waits for them, and re-layouts  16.6 us (12%)
  between operations  15.8 us (11%)
  waiting for transfers between devices  14.6 us (10%)
  other arithmetic  12.4 us (9%)
  starting transfers between devices  11.9 us (8%)
    unnamed x1, blocking collectives  26.1 us
    psum x1, blocking collectives, body(): grad_rate = -lax.psum(rate_total, 'seq')  19.4 us
    psum x1, waiting for transfers between devices, body(): grad_input_map = lax.psum(grad_b_list[0], 'head')  9.15 us
    all_to_all x1, starting transfers between devices, body(): lax.all_to_all(sliced, 'seq', split_axis=1, concat_axis=1, tiled=True)  7.31 us
    mul x8, local copies, waits for them, and re-layouts, backward_step(): return (grad_piece + gain_piece[:, None] * running, running)  5.48 us
    all_to_all x1, waiting for transfers between devices, body(): lax.all_to_all(jnp.transpose(exclusive, (1, 0, 2)), 'seq', split_axis=1,...  5.48 us
    dot_general x1, matrix products, prepare(): jnp.einsum('shp,uhp->hsu', x_block, grad_block, preferred_element_type=jn...  5.34 us
    unnamed x51, local copies, waits for them, and re-layouts  5.26 us
  transfers between devices with their start and end apart: 3, of which 2 were waited for; matrix products, arithmetic and copies ran while one was open for 15% of the time, Pallas kernels for 0%

commit v1 on v0

--- a/solution.py
+++ b/solution.py
@@ -139,7 +139,8 @@
         rate_total = rate_part
         carried = prepared[1] + prepared[0][:, None, None] * carried
     grad_inputs = grad_x_list[0]
-    grad_input_map = lax.psum(grad_b_list[0], "head")
+    packet = grad_b_list[0]
+    grad_input_map = jnp.sum(jax.lax.all_gather(packet, "head"), 0)
     grad_rate = -lax.psum(rate_total, "seq")
     return (grad_inputs, grad_input_map, grad_rate)
 

time: 142 us -> 130 us (0.915)
  between operations: 15.8 us -> 2.25 us
  waiting for transfers between devices: 14.6 us -> 5.55 us
  blocking collectives: 45.5 us -> 51.4 us
  other arithmetic: 12.4 us -> 15.3 us
  matrix products: 24 us -> 26.5 us
    psum x1 -> x0, waiting for transfers between devices: 9.15 us -> none  [body(): grad_input_map = lax.psum(grad_b_list[0], 'head')]
    all_gather x0 -> x1, blocking collectives: none -> 7.17 us  [body(): grad_input_map = jnp.sum(jax.lax.all_gather(packet, 'head'), 0)]
    unnamed x51 -> x40, local copies, waits for them, and re-layouts: 5.26 us -> 4.94 us
  transfers between devices with their start and end apart: 3 -> 2, of which waited for: 2 -> 1; matrix products, arithmetic and copies ran while one was open for 15% -> 16% of each run, Pallas kernels for 0% -> 0%
where the time goes in v1:
time: 130 us; the launch traced here: 129 us
  blocking collectives  51.4 us (40%)
  matrix products  26.5 us (20%)
  local copies, waits for them, and re-layouts  16.3 us (13%)
  other arithmetic  15.3 us (12%)
  starting transfers between devices  11.8 us (9%)
  waiting for transfers between devices  5.55 us (4%)
  between operations  2.25 us (2%)
    unnamed x1, blocking collectives  24.8 us
    psum x1, blocking collectives, body(): grad_rate = -lax.psum(rate_total, 'seq')  19.4 us
    all_to_all x1, starting transfers between devices, body(): lax.all_to_all(sliced, 'seq', split_axis=1, concat_axis=1, tiled=True)  7.31 us
    all_gather x1, blocking collectives, body(): grad_input_map = jnp.sum(jax.lax.all_gather(packet, 'head'), 0)  7.17 us
    all_to_all x1, waiting for transfers between devices, body(): lax.all_to_all(jnp.transpose(exclusive, (1, 0, 2)), 'seq', split_axis=1,...  5.55 us
    mul x8, local copies, waits for them, and re-layouts, backward_step(): return (grad_piece + gain_piece[:, None] * running, running)  5.46 us
    dot_general x1, matrix products, prepare(): jnp.einsum('hsu,un->hsn', paired, c_block, preferred_element_type=jnp.flo...  5.42 us
    dot_general x1, matrix products, prepare(): jnp.einsum('shp,uhp->hsu', x_block, grad_block, preferred_element_type=jn...  5.34 us
  transfers between devices with their start and end apart: 2, of which 1 were waited for; matrix products, arithmetic and copies ran while one was open for 16% of the time, Pallas kernels for 0%

profile of v1, /device:TPU:0, one launch (start us, length us, event | category | flops | bytes accessed | tf_op | source)
XLA Modules:
  0.0 129.3 jit_solution(13751108665343851605)
XLA Ops:
  1.4 0.7 neg.7
  2.1 0.8 reshape.290
  2.8 0.6 reduce-window.6
  3.4 0.2 slice_reduce_fusion
  3.8 0.6 iota_compare_fusion.1
  4.4 0.8 select_reduce_fusion
  5.2 0.9 copy.48
  6.2 1.4 %copy.47 = bf16[256,1280]{0,1:T(8,128)(2,1)S(1)} copy(bf16[256,1280]{1,0:T(8,128)(2,1)} %param.15) | data formatting | bytes 1310720 | tf_op args[5]
  7.6 1.7 %fusion.31 = f32[20,64,128]{2,1,0:T(8,128)S(1)} fusion(bf16[256,20,64]{0,2,1:T(8,128)(2,1)S(1)} %bitcast.82, f32[256,128]{0,1:T(8,128)S(1)} %copy.48, f32[20,256]{1,0:T(8,128)S(1)} %get-tuple-element.155, f32[20]{0:T(128)S(1)} %broadcast_multiply_fusion.1), kind=kOutput, calls=%fused_computation.38 | convolution fusion | flops 504135680 | bytes 1462352 | tf_op jit(solution)/shard_map/hun,uhp->hpn/dot_general | solution.py:34
  9.3 0.1 reshape.293
  9.4 1.3 copy.50
  10.7 7.3 %all-to-all-start = ((f32[20,8,1024]{2,0,1:T(8,128)}), f32[20,8,1024]{2,0,1:T(8,128)S(1)}, u32[]{:S(2)}, u32[]{:S(2)}) async-start(f32[20,8,1024]{2,0,1:T(8,128)} %copy.50), calls=%async_computation | async-start | bytes 1572864 | tf_op jit(solution)/shard_map/all_to_all | solution.py:116
  18.0 1.3 %dynamic-slice = u32[1]{0:T(128)} dynamic-slice(u32[32]{0:T(128)} %constant.57, u32[]{:T(128)S(6)} %add.58), dynamic_slice_sizes={1} | dynamic-slice | bytes 12
  20.0 0.9 dynamic-update-slice
  20.8 24.8 %all-reduce = f32[160]{0:T(256)S(1)} all-reduce(f32[160]{0:T(256)S(1)} %dynamic-update-slice), channel_id=2, replica_groups=mesh['seq'=8,'head'=4] {'seq'}, use_global_device_ids=true, to_apply=%add | all-reduce | flops 160 | bytes 1280
  45.7 0.7 reshape.297
  46.3 1.5 %convert_element_type.21 = f32[256,128]{1,0:T(8,128)} convert(bf16[256,128]{1,0:T(8,128)(2,1)} %param.13) | non-fusion elementwise | flops 32768 | bytes 196608 | tf_op jit(solution)/shard_map/convert_element_type | solution.py:58
  47.8 0.2 copy.52
  48.1 0.1 squeeze.25
  48.2 0.6 compare_bitcast_fusion
  48.8 0.8 slice_reduce_fusion.1
  49.5 1.5 %fusion.37 = pred[256,256]{1,0:T(8,128)(4,1)} fusion(pred[256]{0:T(512)(128)(4,1)} %copy-done.9), kind=kLoop, calls=%fused_computation.42 | loop fusion | flops 196608 | bytes 65792 | tf_op jit(solution)/shard_map/and | solution.py:16
  51.0 1.8 %fusion.43 = f32[256,256]{1,0:T(8,128)} fusion(bf16[256,128]{1,0:T(8,128)(2,1)} %param.13, bf16[256,128]{1,0:T(8,128)(2,1)} %param.14), kind=kOutput, calls=%fused_computation.64 | convolution fusion | flops 16777216 | bytes 393216 | tf_op jit(solution)/shard_map/dot_general | solution.py:19
  52.8 1.0 broadcast_in_dim.97
  53.8 11.4 %while.17 = (s32[]{:T(128)}, f32[20,1024]{1,0:T(8,128)S(1)}, f32[8,20,1024]{2,1,0:T(8,128)}, f32[8,20,1024]{2,1,0:T(8,128)S(1)}, f32[8,20]{1,0:T(8,128)}, /*index=5*/s32[]{:T(128)}, s32[]{:T(128)}, s32[]{:T(128)}) while((s32[]{:T(128)}, f32[20,1024]{1,0:T(8,128)S(1)}, f32[8,20,1024]{2,1,0:T(8,128)}, f32[8,20,1024]{2,1,0:T(8,128)S(1)}, ...), condition=%wide.region_3.4_spmd.clone, body=%wide.region_2.3_spmd.clone.sunk | while | flops 81924 | bytes 426352 | solution.py:118
  53.8 0.7 fusion.55
  54.4 0.6 bitcast_dynamic-update-slice_fusion.2
  55.1 0.1 bitcast_add_fusion.2
  55.2 0.7 fusion.55
  55.9 0.6 bitcast_dynamic-update-slice_fusion.2
  56.5 0.1 bitcast_add_fusion.2
  56.6 0.7 fusion.55
  57.3 0.6 bitcast_dynamic-update-slice_fusion.2
  57.9 0.1 bitcast_add_fusion.2
  58.0 0.7 fusion.55
  58.7 0.6 bitcast_dynamic-update-slice_fusion.2
  59.4 0.1 bitcast_add_fusion.2
  59.5 0.7 fusion.55
  60.1 0.7 bitcast_dynamic-update-slice_fusion.2
  60.8 0.1 bitcast_add_fusion.2
  60.9 0.7 fusion.55
  61.6 0.6 bitcast_dynamic-update-slice_fusion.2
  62.2 0.1 bitcast_add_fusion.2
  62.3 0.7 fusion.55
  63.0 0.6 bitcast_dynamic-update-slice_fusion.2
  63.6 0.1 bitcast_add_fusion.2
  63.7 0.7 fusion.55
  64.4 0.6 bitcast_dynamic-update-slice_fusion.2
  65.2 4.5 %all-to-all-start.1 = ((f32[20,8,1024]{2,0,1:T(8,128)}), f32[20,8,1024]{2,0,1:T(8,128)S(1)}, u32[]{:S(2)}, u32[]{:S(2)}) async-start(f32[20,8,1024]{2,0,1:T(8,128)} %bitcast.8), calls=%async_computation.1 | async-start | bytes 1572864 | tf_op jit(solution)/shard_map/all_to_all | solution.py:124
  69.7 2.8 %multiply_reduce_fusion.1 = f32[20,256]{1,0:T(8,128)} fusion(bf16[256,20,64]{0,2,1:T(8,128)(2,1)S(1)} %bitcast.83, f32[256,128]{0,1:T(8,128)} %copy-done.6, f32[1,20,64,128]{3,2,1,0:T(8,128)S(1)} %copy-done.1), kind=kOutput, calls=%fused_computation.17 | convolution fusion | flops 504622080 | bytes 1462272 | tf_op jit(solution)/shard_map/uhp,hpn->hun/dot_general | solution.py:35
  72.5 3.7 %fusion.21 = f32[256,20,64]{0,2,1:T(8,128)} fusion(bf16[256,20,64]{0,2,1:T(8,128)(2,1)S(1)} %bitcast.84, f32[256,256]{1,0:T(8,128)} %fusion.43, f32[20,256]{1,0:T(8,128)S(1)} %get-tuple-element.156, pred[256,256]{1,0:T(8,128)(4,1)} %fusion.37), kind=kOutput, calls=%fused_computation.29 | convolution fusion | flops 174325760 | bytes 2314240 | tf_op jit(solution)/shard_map/hsu,uhp->shp/dot_general | solution.py:24
  76.3 5.3 %multiply_reduce_fusion = (f32[20]{0:T(128)}, f32[20,256,256]{2,1,0:T(8,128)}) fusion(f32[20,256]{1,0:T(8,128)S(1)} %bitcast.88, f32[20,256]{1,0:T(8,128)S(1)} %copy-done.5, f32[256,256]{1,0:T(8,128)S(1)} %copy-done.3, f32[20,256]{1,0:T(8,128)S(1)} %get-tuple-element.156, pred[256,256]{1,0:T(8,128)(4,1)S(1)} %copy-done.7, ...), kind=kOutput, calls=%fused_computation.4 | convolution fusion | flops 179568624 | bytes 6942800 | tf_op jit(solution)/shard_map/shp,uhp->hsu/dot_general | solution.py:20
  81.6 5.5 %all-to-all-done.1 = f32[20,8,1024]{2,0,1:T(8,128)S(1)} async-done(((f32[20,8,1024]{2,0,1:T(8,128)}), f32[20,8,1024]{2,0,1:T(8,128)S(1)}, u32[]{:S(2)}, u32[]{:S(2)}) %all-to-all-start.1) | async-done | bytes 655392 | tf_op jit(solution)/shard_map/all_to_all | solution.py:124
  87.2 1.1 multiply_reduce_fusion.2
  88.2 0.1 reshape.294
  88.3 3.7 %fusion.9 = (f32[20,256]{1,0:T(8,128)S(1)}, f32[20,128,256]{1,2,0:T(8,128)}) fusion(f32[256,128]{1,0:T(8,128)} %convert_element_type.21, f32[20,64,128]{2,1,0:T(8,128)S(1)} %reshape.294, bf16[256,20,64]{0,2,1:T(8,128)(2,1)S(1)} %bitcast.78), kind=kOutput, calls=%fused_computation.16 | convolution fusion | flops 504622080 | bytes 4083712 | tf_op jit(solution)/shard_map/shp,hpn->hsn/dot_general | solution.py:61
  92.0 0.9 multiply_reduce_fusion.4
  93.0 2.0 %fusion.25 = bf16[256,20,64]{0,2,1:T(8,128)(2,1)S(1)} fusion(f32[256,20,64]{0,2,1:T(8,128)} %fusion.21, f32[20,64,128]{2,1,0:T(8,128)S(1)} %reshape.294, f32[256,20]{0,1:T(8,128)S(1)} %get-tuple-element.154, f32[256,20]{0,1:T(8,128)S(1)} %bitcast.90, bf16[256,128]{1,0:T(8,128)(2,1)S(1)} %copy-done.2), kind=kOutput, calls=%fused_computation.34 | convolution fusion | flops 504627200 | bytes 2727936 | tf_op jit(solution)/shard_map/sn,hpn->shp/dot_general | solution.py:60
  95.0 1.1 copy.55
  96.1 19.4 %psum.7 = f32[20]{0:T(128)S(1)} all-reduce(f32[20]{0:T(128)S(1)} %multiply_add_fusion), channel_id=1, replica_groups=mesh['seq'=8,'head'=4] {'seq'}, use_global_device_ids=true, to_apply=%region_12.13 | all-reduce | flops 20 | bytes 160 | tf_op jit(solution)/shard_map/psum | solution.py:144
  115.5 0.5 neg.8
  116.0 5.4 %fusion.8 = f32[256,128]{1,0:T(8,128)S(1)} fusion(f32[20,128,256]{1,2,0:T(8,128)} %get-tuple-element.158, f32[20,256]{1,0:T(8,128)S(1)} %get-tuple-element.153, f32[20,256]{1,0:T(8,128)S(1)} %copy-done.5, f32[20,256,256]{2,1,0:T(8,128)} %get-tuple-element.160, f32[20,256]{1,0:T(8,128)S(1)} %get-tuple-element.156, pred[256,256]{1,0:T(8,128)(4,1)S(1)} %copy-done.8, ...), kind=kOutput, calls=%fused_computation.15 | convolution fusion | flops 344686592 | bytes 8187904 | tf_op jit(solution)/shard_map/hsu,un->hsn/dot_general | solution.py:25
  121.4 7.2 %all-gather.1 = f32[1024,128]{1,0:T(8,128)S(1)} all-gather(f32[256,128]{1,0:T(8,128)S(1)} %fusion.8), channel_id=3, replica_groups=mesh['seq'=8,'head'=4] {'head'}, dimensions={0}, use_global_device_ids=true | all-gather | bytes 655360 | tf_op jit(solution)/shard_map/all_gather | solution.py:143
  128.6 0.7 reduce_sum.73
  (46 shorter events, 0.4 us)
Async XLA Ops:
  0.6 47.2 %copy-start = (bf16[256,1280]{1,0:T(8,128)(2,1)S(1)}, bf16[256,1280]{1,0:T(8,128)(2,1)}, u32[]{:S(2)}) copy-start(bf16[256,1280]{1,0:T(8,128)(2,1)} %param.10) | copy-start | bytes 1966084
  0.6 47.4 %copy-start.1 = (f32[1,20,64,128]{3,2,1,0:T(8,128)S(1)}, f32[1,20,64,128]{3,2,1,0:T(8,128)}, u32[]{:S(2)}) copy-start(f32[1,20,64,128]{3,2,1,0:T(8,128)} %param.16) | copy-start | bytes 1966084
  2.1 2.4 %copy-start.13 = (f32[20]{0:T(128)}, f32[20]{0:T(128)S(1)}, u32[]{:S(2)}) copy-start(f32[20]{0:T(128)S(1)} %neg.7) | copy-start | bytes 244
  4.3 13.6 %copy-start.9 = (pred[256]{0:T(512)(128)(4,1)}, pred[256]{0:T(512)(128)(4,1)S(1)}, u32[]{:S(2)}) copy-start(pred[256]{0:T(512)(128)(4,1)S(1)} %get-tuple-element.161) | copy-start | bytes 772
  5.2 12.8 %copy-start.10 = (f32[20]{0:T(128)}, f32[20]{0:T(128)S(1)}, u32[]{:S(2)}) copy-start(f32[20]{0:T(128)S(1)} %get-tuple-element.140) | copy-start | bytes 244
  6.2 1.4 %copy-start.6 = (f32[256,128]{0,1:T(8,128)}, f32[256,128]{0,1:T(8,128)S(1)}, u32[]{:S(2)}) copy-start(f32[256,128]{0,1:T(8,128)S(1)} %copy.48) | copy-start | bytes 393220
  10.7 42.1 %all-to-all-start = ((f32[20,8,1024]{2,0,1:T(8,128)}), f32[20,8,1024]{2,0,1:T(8,128)S(1)}, u32[]{:S(2)}, u32[]{:S(2)}) async-start(f32[20,8,1024]{2,0,1:T(8,128)} %copy.50), calls=%async_computation | async-start | bytes 1572864 | tf_op jit(solution)/shard_map/all_to_all | solution.py:116
  65.2 22.0 %all-to-all-start.1 = ((f32[20,8,1024]{2,0,1:T(8,128)}), f32[20,8,1024]{2,0,1:T(8,128)S(1)}, u32[]{:S(2)}, u32[]{:S(2)}) async-start(f32[20,8,1024]{2,0,1:T(8,128)} %bitcast.8), calls=%async_computation.1 | async-start | bytes 1572864 | tf_op jit(solution)/shard_map/all_to_all | solution.py:124
  72.5 3.7 %copy-start.3 = (f32[256,256]{1,0:T(8,128)S(1)}, f32[256,256]{1,0:T(8,128)}, u32[]{:S(2)}) copy-start(f32[256,256]{1,0:T(8,128)} %fusion.43) | copy-start | bytes 786436
  72.5 3.7 %copy-start.5 = (f32[20,256]{1,0:T(8,128)S(1)}, f32[20,256]{1,0:T(8,128)}, u32[]{:S(2)}) copy-start(f32[20,256]{1,0:T(8,128)} %param.11) | copy-start | bytes 61444
  72.5 3.7 %copy-start.7 = (pred[256,256]{1,0:T(8,128)(4,1)S(1)}, pred[256,256]{1,0:T(8,128)(4,1)}, u32[]{:S(2)}) copy-start(pred[256,256]{1,0:T(8,128)(4,1)} %fusion.37) | copy-start | bytes 196612
  81.6 10.4 %copy-start.11 = (f32[20]{0:T(128)S(1)}, f32[20]{0:T(128)}, u32[]{:S(2)}) copy-start(f32[20]{0:T(128)} %copy-done.10) | copy-start | bytes 244
  81.6 10.4 %copy-start.12 = (f32[20]{0:T(128)S(1)}, f32[20]{0:T(128)}, u32[]{:S(2)}) copy-start(f32[20]{0:T(128)} %slice_reduce_fusion.1) | copy-start | bytes 244
  81.6 11.3 %copy-start.2 = (bf16[256,128]{1,0:T(8,128)(2,1)S(1)}, bf16[256,128]{1,0:T(8,128)(2,1)}, u32[]{:S(2)}) copy-start(bf16[256,128]{1,0:T(8,128)(2,1)} %param.13) | copy-start | bytes 196612
  88.2 6.8 %copy-start.14 = (f32[20]{0:T(128)S(1)}, f32[20]{0:T(128)}, u32[]{:S(2)}) copy-start(f32[20]{0:T(128)} %get-tuple-element.151) | copy-start | bytes 244
  88.2 6.8 %copy-start.15 = (f32[20]{0:T(128)S(1)}, f32[20]{0:T(128)}, u32[]{:S(2)}) copy-start(f32[20]{0:T(128)} %get-tuple-element.159) | copy-start | bytes 244
  88.2 27.8 %copy-start.4 = (bf16[256,128]{1,0:T(8,128)(2,1)S(1)}, bf16[256,128]{1,0:T(8,128)(2,1)}, u32[]{:S(2)}) copy-start(bf16[256,128]{1,0:T(8,128)(2,1)} %param.14) | copy-start | bytes 196612
  88.2 27.8 %copy-start.8 = (pred[256,256]{1,0:T(8,128)(4,1)S(1)}, pred[256,256]{1,0:T(8,128)(4,1)}, u32[]{:S(2)}) copy-start(pred[256,256]{1,0:T(8,128)(4,1)} %fusion.37) | copy-start | bytes 196612
